TPU v7x, 32 devices: a whole 2x2x4 slice. The times are simulated.
32 devices in a mesh: seq: 8 (over z, y), head: 4 (over x, core).
Axes of the slice: x: 2, y: 2, z: 4, core: 2. Of those that a mesh axis runs over, the one named last changes fastest.
Arguments:
- hidden_states: bfloat16 [8, 512, 3584], P(None, 'seq', 'head'), may hold values from -6 to 6
- boundary: int32 [8, 64], replicated, may hold values from 0 to 511, as said below
- valid: int32 [8, 64], replicated, may hold values from 0 to 1, as said below
- pairs: int32 [8, 2], replicated, may hold values from 0 to 7, as said below
- w_first: bfloat16 [3584, 4096], P('seq', 'head'), may hold values from -0.09375 to 0.09375
- b_first: float32 [4096], P('head'), may hold values from -3 to 3
- w_second: float32 [4096], P('head'), may hold values from -0.09375 to 0.09375
Outputs:
- step_reward: float32 [8, 64], replicated
- trace_score: float32 [8], replicated
- margin: float32 [8], replicated
Inputs may be any that keep to these rules, and one draw needn't show every extreme that they name: Within a trace the 64 boundary positions are distinct and increasing. In each trace the ones come first; every trace has 16 to 64 valid steps. `pairs`: the two traces of a pair differ.
All inputs are finite; a program needn't handle non-finite values.
Results may differ from a plain program's by a relative error of at most 0.0003.
Values may be sent and summed in bfloat16 or wider, within the bound.
A program may use at most 64 MiB of HBM per device.

v0:
```python
import jax
import jax.numpy as jnp
from jax import lax
from jax.sharding import PartitionSpec as P


def score_rows(rows, w_first, b_first, w_second):
    pre = jnp.dot(
        rows, lax.all_gather(w_first, "seq", axis=0, tiled=True), preferred_element_type=jnp.float32
    )
    return jnp.sum(jnp.maximum(pre + b_first, 0.0) * w_second, axis=-1)


def per_device(hidden_states, boundary, valid, pairs, w_first, b_first, w_second):
    traces, tok_dev, quarter = hidden_states.shape
    offset = lax.axis_index("seq") * tok_dev
    positions = offset + jnp.arange(tok_dev, dtype=jnp.int32)
    hits = boundary[:, :, None] == positions[None, None, :]
    whole = lax.all_gather(hidden_states, "head", axis=2, tiled=True)
    token_logit = score_rows(
        whole.reshape(traces * tok_dev, whole.shape[2]), w_first, b_first, w_second
    )
    token_logit = token_logit.reshape(traces, tok_dev)
    partial_logit = jnp.sum(jnp.where(hits, token_logit[:, None, :], 0.0), axis=2)
    logit = lax.psum(partial_logit, ("seq", "head"))
    live = valid == 1
    step_reward = jnp.where(live, logit, jnp.float32(0.0))
    trace_score = jnp.min(jnp.where(live, logit, jnp.float32(1e30)), axis=1)
    trace_ids = jnp.arange(traces, dtype=jnp.int32)[None, :]
    winner = jnp.sum(jnp.where(pairs[:, 0:1] == trace_ids, trace_score[None, :], 0.0), axis=1)
    loser = jnp.sum(jnp.where(pairs[:, 1:2] == trace_ids, trace_score[None, :], 0.0), axis=1)
    return (step_reward, trace_score, winner - loser)


def solution(mesh):
    placed = (P(None, "seq", "head"), P(), P(), P(), P("seq", "head"), P("head"), P("head"))
    return jax.shard_map(
        per_device, mesh=mesh, in_specs=placed, out_specs=(P(), P(), P()), check_vma=False
    )
```

profile of v0, /device:TPU:0, one launch (start us, length us, event | category | flops | bytes accessed | tf_op | source)
XLA Modules:
  0.0 212.7 jit_solution(10916989333486681788)
XLA Ops:
  7.2 0.0 all-gather.3.cloned.1.call-start
  7.2 0.7 all-gather.3.cloned.1.call-update
  7.9 0.0 all-gather.5.cloned.1.call-start
  7.9 0.7 all-gather.5.cloned.1.call-update
  8.7 0.8 slice_bitcast_fusion.1
  9.4 34.3 %all-gather.3.cloned.1.call-done = bf16[8,64,3584]{2,1,0:T(8,128)(2,1)} async-done(((bf16[8,64,896]{2,1,0:T(8,128)(2,1)}), bf16[8,64,3584]{2,1,0:T(8,128)(2,1)}) %all-gather.3.cloned.1.call-update) | async-done | bytes 3670032 | tf_op jit(solution)/shard_map/all_gather | solution.py:19
  43.8 113.7 %all-gather.5.cloned.1.call-done = bf16[3584,1024]{1,0:T(8,128)(2,1)} async-done(((bf16[448,1024]{1,0:T(8,128)(2,1)}), bf16[3584,1024]{1,0:T(8,128)(2,1)}) %all-gather.5.cloned.1.call-update) | async-done | bytes 7340048 | tf_op jit(solution)/shard_map/all_gather | solution.py:9
  157.5 0.0 copy-start
  157.5 0.0 copy-start.1
  157.5 8.2 %multiply_reduce_fusion = f32[512]{0:T(512)S(1)} fusion(bf16[512,3584]{1,0:T(8,128)(2,1)} %bitcast.7, bf16[3584,1024]{1,0:T(8,128)(2,1)} %all-gather.5.cloned.1.call-done, f32[1024]{0:T(1024)} %param.13, f32[1024]{0:T(1024)} %param.12), kind=kOutput, calls=%fused_computation | convolution fusion | flops 3760193024 | bytes 11020288 | tf_op jit(solution)/shard_map/dot_general | solution.py:8
  165.7 0.1 broadcast_in_dim.44
  165.7 0.0 copy-done
  165.7 0.3 select_reduce_fusion
  166.0 38.4 %psum.7 = f32[8,64]{1,0:T(8,128)S(1)} all-reduce(f32[8,64]{1,0:T(8,128)S(1)} %select_reduce_fusion), channel_id=1, replica_groups=mesh['seq'=8,'head'=4] {'seq','head'}, use_global_device_ids=true, to_apply=%region_2.3 | all-reduce | flops 512 | bytes 4096 | tf_op jit(solution)/shard_map/psum | solution.py:25
  204.4 0.0 copy-done.1
  204.4 0.1 select_reduce_fusion.3
  204.5 0.0 copy-start.2
  204.5 0.6 broadcast_select_fusion
  205.1 0.2 select_reduce_fusion.1
  205.4 0.5 sub.3
  205.9 0.0 copy-done.2
  (1 shorter events, 0.0 us)
Async XLA Ops:
  7.2 36.6 %all-gather.3.cloned.1.call-start = ((), (), s32[]{:S(2)}) async-start(), calls=%async_computation | async-start | bytes 4587520 | tf_op jit(solution)/shard_map/all_gather | solution.py:19
  7.9 149.6 %all-gather.5.cloned.1.call-start = ((), (), s32[]{:S(2)}) async-start(), calls=%async_computation.1 | async-start | bytes 8257536 | tf_op jit(solution)/shard_map/all_gather | solution.py:9
  157.5 8.3 %copy-start = (s32[8,64]{1,0:T(8,128)S(1)}, s32[8,64]{1,0:T(8,128)}, u32[]{:S(2)}) copy-start(s32[8,64]{1,0:T(8,128)} %param.8) | copy-start | bytes 6148
  157.5 47.0 %copy-start.1 = (s32[8,64]{1,0:T(8,128)S(1)}, s32[8,64]{1,0:T(8,128)}, u32[]{:S(2)}) copy-start(s32[8,64]{1,0:T(8,128)} %param.9) | copy-start | bytes 6148
  204.5 1.3 copy-start.2
Sparse Core Ops, SparseCore 0:
  9.5 34.1 all-gather.2
  45.9 111.4 all-gather.4
where the time goes:
time: 213 us
  waiting for transfers between devices  149 us (70%)
  blocking collectives  38.4 us (18%)
  between operations  14.1 us (7%)
  matrix products  8.19 us (4%)
    all_gather x1, waiting for transfers between devices, score_rows(): lax.all_gather(w_first, 'seq', axis=0, tiled=True)  114 us
    psum x1, blocking collectives, per_device(): logit = lax.psum(partial_logit, ('seq', 'head'))  38.4 us
    all_gather x1, waiting for transfers between devices, per_device(): whole = lax.all_gather(hidden_states, 'head', axis=2, tiled=True)  34.3 us
    dot_general x1, matrix products, score_rows(): jnp.dot(rows, lax.all_gather(w_first, 'seq', axis=0, tiled=True), preferr...  8.19 us
  transfers between devices with their start and end apart: 2, of which 2 were waited for; matrix products, arithmetic and copies ran while one was open for 0% of the time, Pallas kernels for 0%

commit v1 on v0

--- a/solution.py
+++ b/solution.py
@@ -16,7 +16,12 @@
     offset = lax.axis_index("seq") * tok_dev
     positions = offset + jnp.arange(tok_dev, dtype=jnp.int32)
     hits = boundary[:, :, None] == positions[None, None, :]
-    whole = lax.all_gather(hidden_states, "head", axis=2, tiled=True)
+    ring = [hidden_states]
+    for hop in range(3):
+        ring.append(lax.ppermute(ring[-1], "head", [(dev, (dev + 1) % 4) for dev in range(4)]))
+    whole = jnp.roll(
+        jnp.concatenate(ring[::-1], axis=2), (lax.axis_index("head") + 1) * ring[0].shape[2], axis=2
+    )
     token_logit = score_rows(
         whole.reshape(traces * tok_dev, whole.shape[2]), w_first, b_first, w_second
     )

time: 213 us -> 180 us (0.85)
  waiting for transfers between devices: 149 us -> 106 us
  local copies, waits for them, and re-layouts: 0.85 us -> 10.4 us
    all_gather x1, waiting for transfers between devices: 114 us -> 67.4 us  [score_rows(): lax.all_gather(w_first, 'seq', axis=0, tiled=True)]
    ppermute x0 -> x3, waiting for transfers between devices: none -> 38.1 us  [per_device(): lax.ppermute(ring[-1], 'head', [(dev, (dev + 1) % 4) for dev in range(4)])]
    all_gather x1 -> x0, waiting for transfers between devices: 34.3 us -> none  [per_device(): whole = lax.all_gather(hidden_states, 'head', axis=2, tiled=True)]
    dynamic_slice x0 -> x1, local copies, waits for them, and re-layouts: none -> 4.72 us  [per_device(): jnp.roll(jnp.concatenate(ring[::-1], axis=2), (lax.axis_index('head') + 1...]
    unnamed x6 -> x19, local copies, waits for them, and re-layouts: 0.01 us -> 4.67 us
  transfers between devices with their start and end apart: 2 -> 4, of which waited for: 2 -> 4; matrix products, arithmetic and copies ran while one was open for 0% -> 6% of each run, Pallas kernels for 0% -> 0%
where the time goes in v1:
time: 180 us
  waiting for transfers between devices  106 us (59%)
  blocking collectives  38.4 us (21%)
  between operations  14.1 us (8%)
  local copies, waits for them, and re-layouts  10.4 us (6%)
  matrix products  8.26 us (5%)
    all_gather x1, waiting for transfers between devices, score_rows(): lax.all_gather(w_first, 'seq', axis=0, tiled=True)  67.4 us
    psum x1, blocking collectives, per_device(): logit = lax.psum(partial_logit, ('seq', 'head'))  38.4 us
    ppermute x3, waiting for transfers between devices, per_device(): lax.ppermute(ring[-1], 'head', [(dev, (dev + 1) % 4) for dev in range(4)])  38.1 us
    dot_general x1, matrix products, score_rows(): jnp.dot(rows, lax.all_gather(w_first, 'seq', axis=0, tiled=True), preferr...  8.26 us
    dynamic_slice x1, local copies, waits for them, and re-layouts, per_device(): jnp.roll(jnp.concatenate(ring[::-1], axis=2), (lax.axis_index('head') + 1...  4.72 us
    unnamed x19, local copies, waits for them, and re-layouts  4.67 us
  transfers between devices with their start and end apart: 4, of which 4 were waited for; matrix products, arithmetic and copies ran while one was open for 6% of the time, Pallas kernels for 0%

profile of v1, /device:TPU:0, one launch (start us, length us, event | category | flops | bytes accessed | tf_op | source)
XLA Modules:
  0.0 179.8 jit_solution(2447581440533689878)
XLA Ops:
  7.2 0.0 copy-start
  7.2 0.0 all-gather.2.cloned.1.call-start
  7.2 0.7 all-gather.2.cloned.1.call-update
  7.9 0.5 collective-permute-start
  8.5 13.2 %collective-permute-done = bf16[8,64,896]{2,1,0:T(8,128)(2,1)S(1)} collective-permute-done((bf16[8,64,896]{2,1,0:T(8,128)(2,1)}, bf16[8,64,896]{2,1,0:T(8,128)(2,1)S(1)}, u32[]{:S(2)}, u32[]{:S(2)}) %collective-permute-start) | collective-permute-done | bytes 917536 | tf_op jit(solution)/shard_map/ppermute | solution.py:21
  21.7 0.0 collective-permute-start.1
  21.7 12.8 %collective-permute-done.1 = bf16[8,64,896]{2,1,0:T(8,128)(2,1)S(1)} collective-permute-done((bf16[8,64,896]{2,1,0:T(8,128)(2,1)S(1)}, bf16[8,64,896]{2,1,0:T(8,128)(2,1)S(1)}, u32[]{:S(2)}, u32[]{:S(2)}) %collective-permute-start.1) | collective-permute-done | bytes 917536 | tf_op jit(solution)/shard_map/ppermute | solution.py:21
  34.5 0.0 collective-permute-start.2
  34.5 0.8 slice_bitcast_fusion.1
  35.2 12.2 %collective-permute-done.2 = bf16[8,64,896]{2,1,0:T(8,128)(2,1)} collective-permute-done((bf16[8,64,896]{2,1,0:T(8,128)(2,1)S(1)}, bf16[8,64,896]{2,1,0:T(8,128)(2,1)}, u32[]{:S(2)}, u32[]{:S(2)}) %collective-permute-start.2) | collective-permute-done | bytes 917536 | tf_op jit(solution)/shard_map/ppermute | solution.py:21
  47.4 1.3 constant_dynamic-update-slice_fusion.7
  48.7 0.2 constant_dynamic-update-slice_fusion.6
  48.9 0.2 constant_dynamic-update-slice_fusion.5
  49.1 1.3 constant_dynamic-update-slice_fusion.4
  50.4 0.0 copy-start.4
  50.4 0.0 copy-start.5
  50.4 1.3 constant_dynamic-update-slice_fusion.3
  51.8 0.2 constant_dynamic-update-slice_fusion.2
  52.0 0.2 constant_dynamic-update-slice_fusion.1
  52.1 0.0 copy-done
  52.1 0.2 constant_dynamic-update-slice_fusion
  52.3 4.7 %constant_dynamic-slice_fusion = bf16[8,64,3584]{2,1,0:T(8,128)(2,1)} fusion(bf16[8,64,7168]{2,1,0:T(8,128)(2,1)S(1)} %constant_dynamic-update-slice_fusion, s32[]{:T(128)S(6)} %select_n.32), kind=kLoop, calls=%fused_computation.20 | loop fusion | bytes 7340036 | tf_op jit(solution)/shard_map/jit(_roll_dynamic)/dynamic_slice | solution.py:22
  57.0 67.4 %all-gather.2.cloned.1.call-done = bf16[3584,1024]{1,0:T(8,128)(2,1)} async-done(((bf16[448,1024]{1,0:T(8,128)(2,1)}), bf16[3584,1024]{1,0:T(8,128)(2,1)}) %all-gather.2.cloned.1.call-update) | async-done | bytes 7340048 | tf_op jit(solution)/shard_map/all_gather | solution.py:9
  124.4 0.0 copy-done.4
  124.4 8.3 %multiply_reduce_fusion = f32[512]{0:T(512)S(1)} fusion(bf16[512,3584]{1,0:T(8,128)(2,1)} %bitcast.7, bf16[3584,1024]{1,0:T(8,128)(2,1)} %all-gather.2.cloned.1.call-done, f32[1024]{0:T(1024)S(1)} %copy-done.4, f32[1024]{0:T(1024)S(1)} %copy-done.5), kind=kOutput, calls=%fused_computation | convolution fusion | flops 3760193024 | bytes 11020288 | tf_op jit(solution)/shard_map/dot_general | solution.py:8
  132.7 0.1 broadcast_in_dim.44
  132.8 0.3 select_reduce_fusion
  133.0 38.4 %psum.7 = f32[8,64]{1,0:T(8,128)S(1)} all-reduce(f32[8,64]{1,0:T(8,128)S(1)} %select_reduce_fusion), channel_id=1, replica_groups=mesh['seq'=8,'head'=4] {'seq','head'}, use_global_device_ids=true, to_apply=%region_2.3 | all-reduce | flops 512 | bytes 4096 | tf_op jit(solution)/shard_map/psum | solution.py:30
  171.5 0.1 select_reduce_fusion.3
  171.6 0.6 broadcast_select_fusion
  172.2 0.2 select_reduce_fusion.1
  172.4 0.5 sub.8
  (8 shorter events, 0.0 us)
Async XLA Ops:
  7.2 45.0 %copy-start = (bf16[8,64,896]{2,1,0:T(8,128)(2,1)S(1)}, bf16[8,64,896]{2,1,0:T(8,128)(2,1)}, u32[]{:S(2)}) copy-start(bf16[8,64,896]{2,1,0:T(8,128)(2,1)} %param.7) | copy-start | bytes 2752516
  7.2 117.2 %all-gather.2.cloned.1.call-start = ((), (), s32[]{:S(2)}) async-start(), calls=%async_computation | async-start | bytes 8257536 | tf_op jit(solution)/shard_map/all_gather | solution.py:9
  7.9 13.7 %collective-permute-start = (bf16[8,64,896]{2,1,0:T(8,128)(2,1)}, bf16[8,64,896]{2,1,0:T(8,128)(2,1)S(1)}, u32[]{:S(2)}, u32[]{:S(2)}) collective-permute-start(bf16[8,64,896]{2,1,0:T(8,128)(2,1)} %param.7), channel_id=1, source_target_pairs={{0,1},{1,2},{2,3},{3,0},{4,5},{5,6},{6,7},{7,4},{8,9},{9,10},{10,1... | collective-permute-start | bytes 2752520 | tf_op jit(solution)/shard_map/ppermute | solution.py:21
  21.7 12.8 %collective-permute-start.1 = (bf16[8,64,896]{2,1,0:T(8,128)(2,1)S(1)}, bf16[8,64,896]{2,1,0:T(8,128)(2,1)S(1)}, u32[]{:S(2)}, u32[]{:S(2)}) collective-permute-start(bf16[8,64,896]{2,1,0:T(8,128)(2,1)S(1)} %collective-permute-done), channel_id=1, source_target_pairs={{0,1},{1,2},{2,3},{3,0},{4,5},{5,6},{6,7},{7,4},{8,9},{9,10},{10,1... | collective-permute-start | bytes 2752520 | tf_op jit(solution)/shard_map/ppermute | solution.py:21
  34.5 12.9 %collective-permute-start.2 = (bf16[8,64,896]{2,1,0:T(8,128)(2,1)S(1)}, bf16[8,64,896]{2,1,0:T(8,128)(2,1)}, u32[]{:S(2)}, u32[]{:S(2)}) collective-permute-start(bf16[8,64,896]{2,1,0:T(8,128)(2,1)S(1)} %collective-permute-done.1), channel_id=1, source_target_pairs={{0,1},{1,2},{2,3},{3,0},{4,5},{5,6},{6,7},{7,4},{8,9},{9,10},{10,1... | collective-permute-start | bytes 2752520 | tf_op jit(solution)/shard_map/ppermute | solution.py:21
  50.4 74.0 %copy-start.4 = (f32[1024]{0:T(1024)S(1)}, f32[1024]{0:T(1024)}, u32[]{:S(2)}) copy-start(f32[1024]{0:T(1024)} %param.13) | copy-start | bytes 12292
  50.4 74.0 %copy-start.5 = (f32[1024]{0:T(1024)S(1)}, f32[1024]{0:T(1024)}, u32[]{:S(2)}) copy-start(f32[1024]{0:T(1024)} %param.12) | copy-start | bytes 12292
  124.4 8.3 %copy-start.1 = (s32[8,64]{1,0:T(8,128)S(1)}, s32[8,64]{1,0:T(8,128)}, u32[]{:S(2)}) copy-start(s32[8,64]{1,0:T(8,128)} %param.8) | copy-start | bytes 6148
  124.4 47.0 %copy-start.2 = (s32[8,64]{1,0:T(8,128)S(1)}, s32[8,64]{1,0:T(8,128)}, u32[]{:S(2)}) copy-start(s32[8,64]{1,0:T(8,128)} %param.9) | copy-start | bytes 6148
  171.6 1.3 copy-start.3
Sparse Core Ops, SparseCore 0:
  10.2 114.1 all-gather.1
